TPU v7x, 16 devices: a 4x2x1 block of a 4x4x8 slice. The times are simulated.
16 devices in a mesh: rep: 4 (over y, z, core), dp: 4 (over x).
Axes of the slice: x: 4, y: 2, z: 1, core: 2. Of those that a mesh axis runs over, the one named last changes fastest.
The devices are a block of a 4x4x8 slice.
Arguments:
- x: bfloat16 [16, 4096, 640], P(('rep', 'dp')), parts along dimension 0
- dy: bfloat16 [16, 4096, 640], P(('rep', 'dp')), parts along dimension 0
- w_gate: bfloat16 [2, 640, 2048], replicated
- w_up: bfloat16 [2, 640, 2048], replicated
- w_down: bfloat16 [2, 2048, 640], replicated
- m_w_gate: float32 [2, 640, 2048], P(None, 'dp')
- m_w_up: float32 [2, 640, 2048], P(None, 'dp')
- m_w_down: float32 [2, 2048, 640], P(None, 'dp')
- v_w_gate: float32 [2, 640, 2048], P(None, 'dp')
- v_w_up: float32 [2, 640, 2048], P(None, 'dp')
- v_w_down: float32 [2, 2048, 640], P(None, 'dp')
Outputs:
- output 1: bfloat16 [8, 640, 2048], P('rep'), parts along dimension 0
- output 2: bfloat16 [8, 640, 2048], P('rep'), parts along dimension 0
- output 3: bfloat16 [8, 2048, 640], P('rep'), parts along dimension 0
- output 4: float32 [8, 640, 2048], P('rep', 'dp'), parts along dimension 0
- output 5: float32 [8, 640, 2048], P('rep', 'dp'), parts along dimension 0
- output 6: float32 [8, 2048, 640], P('rep', 'dp'), parts along dimension 0
- output 7: float32 [8, 640, 2048], P('rep', 'dp'), parts along dimension 0
- output 8: float32 [8, 640, 2048], P('rep', 'dp'), parts along dimension 0
- output 9: float32 [8, 2048, 640], P('rep', 'dp'), parts along dimension 0
There are 4 independent parts. A program takes and returns all parts, laid end to end along the dimension named above; an argument that names none is the same for every part.
All inputs are finite; a program needn't handle non-finite values.
Results may differ from a plain program's by a relative error of at most 0.022.
Values are sent between devices in bfloat16 or wider.
A program may use at most 768 MiB of HBM per device.

v0:
```python
import jax
import jax.numpy as jnp
from jax import lax

NAMES = ("w_gate", "w_up", "w_down")


def matmul(a, w):
    return jnp.dot(a, w, preferred_element_type=jnp.float32).astype(jnp.bfloat16)


def normed(h):
    wide = h.astype(jnp.float32)
    scale = lax.rsqrt(jnp.mean(wide**2, -1, keepdims=True) + 1e-6)
    return (wide * scale).astype(jnp.bfloat16)


def layer(h, w):
    a = normed(h)
    gate = jnp.dot(a, w["w_gate"], preferred_element_type=jnp.float32)
    up = jnp.dot(a, w["w_up"], preferred_element_type=jnp.float32)
    return h + matmul((jax.nn.silu(gate) * up).astype(jnp.bfloat16), w["w_down"])


def adamw(w, m, v, g):
    m = 0.9 * m + 0.1 * g
    v = 0.95 * v + 0.05 * g * g
    step = m * lax.rsqrt(v + 1e-8) + 0.1 * w
    return (w - 0.02 * step).astype(jnp.bfloat16), m, v


def stack(weights, h):
    for number in range(weights["w_gate"].shape[0]):
        h = layer(h, {name: w[number] for name, w in weights.items()})
    return h


def solution(mesh):
    groups = mesh.shape["rep"]

    def step(x, dy, *arrays):
        weights, m, v = (arrays[i : i + 3] for i in (0, 3, 6))
        x, dy = (t.reshape(groups, -1, *t.shape[1:]) for t in (x, dy))

        def of_a_group(x, dy):
            _, back = jax.vjp(lambda w: stack(w, x), dict(zip(NAMES, weights, strict=True)))
            by_weights = back(dy)[0]
            gradients = [by_weights[name].astype(jnp.float32) for name in NAMES]
            new = [adamw(w.astype(jnp.float32), m, v, g) for w, m, v, g in zip(weights, m, v, gradients, strict=True)]
            return tuple(one[which] for which in range(3) for one in new)

        return tuple(t.reshape(-1, *t.shape[2:]) for t in jax.vmap(of_a_group)(x, dy))

    return step
```

profile of v0, /device:TPU:112, one launch (start us, length us, event | category | flops | bytes accessed | tf_op | source)
XLA Modules:
  0.0 788.6 jit_solution(17222628708364900942)
XLA Ops:
  18.8 22.0 %fusion.116 = f32[4096,2048]{1,0:T(8,128)} fusion(bf16[2,640,2048]{2,1,0:T(8,128)(2,1)} %param, bf16[1,4096,640]{2,1,0:T(8,128)(2,1)} %param.2, f32[4096]{0:T(1024)S(1)} %add_rsqrt_fusion), kind=kOutput, calls=%fused_computation.124 | convolution fusion | flops 10745282560 | bytes 41435136 | tf_op jit(solution)/vmap(jvp())/dot_general | solution.py:20
  40.8 19.0 %fusion.114 = f32[4096,2048]{1,0:T(8,128)} fusion(bf16[2,640,2048]{2,1,0:T(8,128)(2,1)} %param.3, bf16[1,4096,640]{2,1,0:T(8,128)(2,1)S(1)} %bitcast.361, f32[4096]{0:T(1024)S(1)} %add_rsqrt_fusion), kind=kOutput, calls=%fused_computation.122 | convolution fusion | flops 10745282560 | bytes 41435136 | tf_op jit(solution)/vmap(jvp())/dot_general | solution.py:21
  59.8 27.6 %fusion.26 = bf16[4096,2048]{1,0:T(8,128)(2,1)} fusion(f32[4096,2048]{1,0:T(8,128)} %fusion.114, f32[4096,2048]{1,0:T(8,128)} %fusion.116), kind=kLoop, calls=%fused_computation.39 | loop fusion | flops 50331648 | bytes 83886080
  87.4 19.0 %fusion.39 = (f32[4096]{0:T(1024)S(1)}, bf16[1,1,4096,640]{2,3,1,0:T(8,128)(2,1)}) fusion(bf16[4096,2048]{1,0:T(8,128)(2,1)} %fusion.26, bf16[2,2048,640]{2,1,0:T(8,128)(2,1)} %param.4, bf16[1,4096,640]{1,2,0:T(8,128)(2,1)} %copy), kind=kOutput, calls=%fused_computation.56 | convolution fusion | flops 10750521344 | bytes 29900800 | tf_op jit(solution)/vmap(jvp())/dot_general | solution.py:9
  107.0 22.2 %fusion.81 = f32[4096,2048]{1,0:T(8,128)} fusion(bf16[1,1,4096,640]{2,3,1,0:T(8,128)(2,1)} %get-tuple-element.10, f32[4096]{0:T(1024)S(1)} %bitcast.370, bf16[2,640,2048]{2,1,0:T(8,128)(2,1)} %param), kind=kOutput, calls=%fused_computation.83 | convolution fusion | flops 10745282560 | bytes 41435136 | tf_op jit(solution)/vmap(jvp())/dot_general | solution.py:20
  129.2 18.9 %fusion.83 = f32[4096,2048]{1,0:T(8,128)} fusion(bf16[1,1,4096,640]{2,3,1,0:T(8,128)(2,1)S(1)} %copy-done.1, f32[4096]{0:T(1024)S(1)} %bitcast.371, bf16[2,640,2048]{2,1,0:T(8,128)(2,1)} %param.3), kind=kOutput, calls=%fused_computation.84 | convolution fusion | flops 10745282560 | bytes 41435136 | tf_op jit(solution)/vmap(jvp())/dot_general | solution.py:21
  148.1 19.9 %convolution_convert_fusion.1 = bf16[4096,2048]{1,0:T(8,128)(2,1)} fusion(bf16[1,4096,640]{2,1,0:T(8,128)(2,1)} %param.5, bf16[2,2048,640]{2,1,0:T(8,128)(2,1)} %param.4), kind=kOutput, calls=%fused_computation.48 | convolution fusion | flops 10745806848 | bytes 24641536 | tf_op jit(solution)/vmap(transpose(jvp()))/dot_general | solution.py:9
  175.9 27.0 %fusion.6 = bf16[4096,2048]{1,0:T(8,128)(2,1)S(1)} fusion(f32[4096,2048]{1,0:T(8,128)} %fusion.81, f32[4096,2048]{1,0:T(8,128)} %fusion.83, bf16[4096,2048]{1,0:T(8,128)(2,1)} %convolution_convert_fusion.1), kind=kLoop, calls=%fused_computation.11 | loop fusion | flops 100663296 | bytes 100663296
  208.7 19.2 %convolution_convert_fusion.3 = bf16[4096,640]{0,1:T(8,128)(2,1)} fusion(bf16[4096,2048]{1,0:T(8,128)(2,1)S(1)} %fusion.6, bf16[2,640,2048]{2,1,0:T(8,128)(2,1)} %param), kind=kOutput, calls=%fused_computation.62 | convolution fusion | flops 10737418240 | bytes 24641536 | tf_op jit(solution)/vmap(transpose(jvp()))/dot_general | solution.py:20
  227.9 26.0 %fusion.41 = (f32[4096]{0:T(1024)S(1)}, bf16[1,1,4096,640]{2,3,1,0:T(8,128)(2,1)}) fusion(bf16[1,1,4096,640]{2,3,1,0:T(8,128)(2,1)} %get-tuple-element.10, bf16[4096,640]{0,1:T(8,128)(2,1)} %convolution_convert_fusion.3, bf16[2,640,2048]{2,1,0:T(8,128)(2,1)} %param.3, bf16[4096,2048]{1,0:T(8,128)(2,1)} %convolution_convert_fusion.1, f32[4096,2048]{1,0:T(8,128)} %fusion.81), kind=kOutput, calls=%fused_computation.58 | convolution fusion | flops 10803474432 | bytes 68698112 | tf_op jit(solution)/vmap(transpose(jvp()))/dot_general | solution.py:21
  253.9 11.9 %fusion.56 = bf16[4096,640]{0,1:T(8,128)(2,1)} fusion(bf16[1,1,4096,640]{2,3,1,0:T(8,128)(2,1)} %get-tuple-element.10, bf16[1,1,4096,640]{2,3,1,0:T(8,128)(2,1)} %get-tuple-element.12, bf16[1,4096,640]{1,2,0:T(8,128)(2,1)} %copy.1, f32[4096]{0:T(1024)S(1)} %bitcast.369, f32[4096]{0:T(1024)S(1)} %bitcast.372), kind=kLoop, calls=%fused_computation.70 | loop fusion | flops 18350080 | bytes 21004288
  265.9 18.7 %convolution_bitcast_fusion = f32[1,2048,640]{2,1,0:T(8,128)} fusion(bf16[4096,2048]{1,0:T(8,128)(2,1)} %fusion.26, bf16[4096,640]{0,1:T(8,128)(2,1)} %fusion.56), kind=kOutput, calls=%fused_computation.80 | convolution fusion | flops 10737418240 | bytes 27262976 | tf_op jit(solution)/vmap(transpose(jvp()))/dot_general | solution.py:9
  284.7 27.7 %fusion.62 = f32[1,2048,640]{2,1,0:T(8,128)} fusion(bf16[1,4096,640]{2,1,0:T(8,128)(2,1)} %param.5, f32[4096,2048]{1,0:T(8,128)} %fusion.83, f32[4096,2048]{1,0:T(8,128)} %fusion.81), kind=kOutput, calls=%fused_computation.77 | convolution fusion | flops 10787749888 | bytes 77594624 | tf_op jit(solution)/vmap(transpose(jvp()))/dot_general | solution.py:9
  312.6 20.0 %convolution_convert_fusion = bf16[4096,2048]{1,0:T(8,128)(2,1)} fusion(bf16[4096,640]{0,1:T(8,128)(2,1)} %fusion.56, bf16[2,2048,640]{2,1,0:T(8,128)(2,1)} %param.4), kind=kOutput, calls=%fused_computation.47 | convolution fusion | flops 10745806848 | bytes 24641536 | tf_op jit(solution)/vmap(transpose(jvp()))/dot_general | solution.py:9
  332.6 23.1 %fusion.70 = f32[1,640,2048]{2,1,0:T(8,128)} fusion(bf16[4096,2048]{1,0:T(8,128)(2,1)} %convolution_convert_fusion, f32[4096,2048]{1,0:T(8,128)} %fusion.116, bf16[1,4096,640]{1,2,0:T(8,128)(2,1)} %copy, f32[4096]{0:T(1024)S(1)} %copy-done.11), kind=kOutput, calls=%fused_computation.79 | convolution fusion | flops 10795614208 | bytes 60833792 | tf_op jit(solution)/vmap(transpose(jvp()))/dot_general | solution.py:21
  356.4 23.5 %fusion.67 = f32[1,640,2048]{2,1,0:T(8,128)} fusion(bf16[4096,2048]{1,0:T(8,128)(2,1)} %convolution_convert_fusion.1, f32[4096,2048]{1,0:T(8,128)} %fusion.81, bf16[1,1,4096,640]{2,3,1,0:T(8,128)(2,1)} %get-tuple-element.10, f32[4096]{0:T(1024)S(1)} %bitcast.373), kind=kOutput, calls=%fused_computation.78 | convolution fusion | flops 10795614208 | bytes 60833792 | tf_op jit(solution)/vmap(transpose(jvp()))/dot_general | solution.py:21
  380.1 17.5 %convolution_bitcast_fusion.1 = f32[1,640,2048]{2,1,0:T(8,128)} fusion(bf16[4096,2048]{1,0:T(8,128)(2,1)} %copy-done, bf16[1,1,4096,640]{2,3,1,0:T(8,128)(2,1)} %get-tuple-element.10, f32[4096]{0:T(1024)S(1)} %bitcast.374), kind=kOutput, calls=%fused_computation.81 | convolution fusion | flops 10745282560 | bytes 27279360 | tf_op jit(solution)/vmap(transpose(jvp()))/dot_general | solution.py:20
  397.8 36.2 %fusion.75 = f32[1,640,2048]{2,1,0:T(8,128)} fusion(f32[4096,2048]{1,0:T(8,128)} %fusion.116, f32[4096,2048]{1,0:T(8,128)} %fusion.114, bf16[4096,2048]{1,0:T(8,128)(2,1)} %convolution_convert_fusion, bf16[1,4096,640]{1,2,0:T(8,128)(2,1)} %copy, f32[4096]{0:T(1024)S(1)} %copy-done.11), kind=kOutput, calls=%fused_computation.82 | convolution fusion | flops 10837557248 | bytes 94388224 | tf_op jit(solution)/vmap(transpose(jvp()))/dot_general | solution.py:20
  447.2 51.7 %reduce-scatter.23.cloned.1.call-done = f32[1,160,2048]{2,1,0:T(8,128)} async-done(((f32[1,640,2048]{2,1,0:T(8,128)}), f32[1,160,2048]{2,1,0:T(8,128)}) %reduce-scatter.23.cloned.1.call-update) | async-done | bytes 1310736
  506.9 45.9 %reduce-scatter.19.cloned.1.call-done = f32[1,160,2048]{2,1,0:T(8,128)} async-done(((f32[1,640,2048]{2,1,0:T(8,128)}), f32[1,160,2048]{2,1,0:T(8,128)}) %reduce-scatter.19.cloned.1.call-update) | async-done | bytes 1310736
  554.2 52.4 %reduce-scatter.21.cloned.1.call-done = f32[1,160,2048]{2,1,0:T(8,128)} async-done(((f32[1,640,2048]{2,1,0:T(8,128)}), f32[1,160,2048]{2,1,0:T(8,128)}) %reduce-scatter.21.cloned.1.call-update) | async-done | bytes 1310736
  614.4 46.2 %all-gather.14.cloned.1.call-done = bf16[1,2,2048,640]{3,2,1,0:T(8,128)(2,1)} async-done(((bf16[1,2,512,640]{3,2,1,0:T(8,128)(2,1)}), bf16[1,2,2048,640]{3,2,1,0:T(8,128)(2,1)}) %all-gather.14.cloned.1.call-update) | async-done | bytes 5242896 | tf_op jit(solution)/reshape | solution.py:52
  660.6 54.9 %all-gather.12.cloned.1.call-done = bf16[1,2,640,2048]{3,2,1,0:T(8,128)(2,1)} async-done(((bf16[1,2,160,2048]{3,2,1,0:T(8,128)(2,1)}), bf16[1,2,640,2048]{3,2,1,0:T(8,128)(2,1)}) %all-gather.12.cloned.1.call-update) | async-done | bytes 5242896 | tf_op jit(solution)/reshape | solution.py:52
  715.5 55.5 %all-gather.10.cloned.1.call-done = bf16[1,2,640,2048]{3,2,1,0:T(8,128)(2,1)} async-done(((bf16[1,2,160,2048]{3,2,1,0:T(8,128)(2,1)}), bf16[1,2,640,2048]{3,2,1,0:T(8,128)(2,1)}) %all-gather.10.cloned.1.call-update) | async-done | bytes 5242896 | tf_op jit(solution)/reshape | solution.py:52
  (77 shorter events, 67.6 us)
Async XLA Ops:
  7.2 428.7 %reduce-scatter.29.cloned.1.call-start = ((), (), s32[]{:S(2)}) async-start(), calls=%async_computation.14 | async-start | bytes 6553600
  10.8 30.0 %slice-start = ((s8[5242880]{0:T(1024)(128)(4,1)}), s8[1048576]{0:T(1024)(128)(4,1)S(1)}, s32[]{:S(2)}) async-start(s8[5242880]{0:T(1024)(128)(4,1)} %bitcast.360), calls=%async_computation.15 | async-start | bytes 2097152
  18.8 22.0 %copy-start.10 = (f32[4096]{0:T(1024)}, f32[4096]{0:T(1024)S(1)}, u32[]{:S(2)}) copy-start(f32[4096]{0:T(1024)S(1)} %add_rsqrt_fusion) | copy-start | bytes 49156
  18.8 22.0 %slice-start.1 = ((s8[5242880]{0:T(1024)(128)(4,1)}), s8[4194304]{0:T(1024)(128)(4,1)S(1)}, s32[]{:S(2)}) async-start(s8[5242880]{0:T(1024)(128)(4,1)} %bitcast.360), calls=%async_computation.16 | async-start | bytes 8388608
  106.4 147.5 %copy-start.8 = (f32[1,1,4096]{2,1,0:T(1,128)}, f32[1,1,4096]{2,1,0:T(1,128)S(1)}, u32[]{:S(2)}) copy-start(f32[1,1,4096]{2,1,0:T(1,128)S(1)} %rsqrt.31) | copy-start | bytes 49156
  107.0 22.2 %copy-start.1 = (bf16[1,1,4096,640]{2,3,1,0:T(8,128)(2,1)S(1)}, bf16[1,1,4096,640]{2,3,1,0:T(8,128)(2,1)}, u32[]{:S(2)}) copy-start(bf16[1,1,4096,640]{2,3,1,0:T(8,128)(2,1)} %get-tuple-element.10) | copy-start | bytes 15728644
  202.9 5.7 copy-start
  227.9 26.0 %copy-start.7 = (f32[4096]{0:T(1024)S(1)}, f32[4096]{0:T(1024)}, u32[]{:S(2)}) copy-start(f32[4096]{0:T(1024)} %copy-done.6) | copy-start | bytes 49156
  284.6 152.7 %reduce-scatter.27.cloned.1.call-start = ((), (), s32[]{:S(2)}) async-start(), calls=%async_computation.13 | async-start | bytes 6553600
  312.5 20.1 %copy-start.11 = (f32[4096]{0:T(1024)S(1)}, f32[4096]{0:T(1024)}, u32[]{:S(2)}) copy-start(f32[4096]{0:T(1024)} %copy-done.10) | copy-start | bytes 49156
  312.5 133.2 %reduce-scatter.25.cloned.1.call-start = ((), (), s32[]{:S(2)}) async-start(), calls=%async_computation.12 | async-start | bytes 6553600
  355.7 0.7 copy-start.9
  355.8 143.2 %reduce-scatter.23.cloned.1.call-start = ((), (), s32[]{:S(2)}) async-start(), calls=%async_computation.11 | async-start | bytes 6553600
  380.0 172.7 %reduce-scatter.19.cloned.1.call-start = ((), (), s32[]{:S(2)}) async-start(), calls=%async_computation.9 | async-start | bytes 6553600
  397.7 208.9 %reduce-scatter.21.cloned.1.call-start = ((), (), s32[]{:S(2)}) async-start(), calls=%async_computation.10 | async-start | bytes 6553600
  434.0 4.7 copy-start.3
  434.0 226.5 %all-gather.14.cloned.1.call-start = ((), (), s32[]{:S(2)}) async-start(), calls=%async_computation.8 | async-start | bytes 6553600 | tf_op jit(solution)/reshape | solution.py:52
  445.1 55.3 %copy-start.4 = (f32[2,160,2048]{2,1,0:T(8,128)S(1)}, f32[2,160,2048]{2,1,0:T(8,128)}, u32[]{:S(2)}) copy-start(f32[2,160,2048]{2,1,0:T(8,128)} %param.8) | copy-start | bytes 7864324
  445.1 270.4 %all-gather.12.cloned.1.call-start = ((), (), s32[]{:S(2)}) async-start(), calls=%async_computation.7 | async-start | bytes 6553600 | tf_op jit(solution)/reshape | solution.py:52
  506.7 101.2 %copy-start.5 = (f32[2,160,2048]{2,1,0:T(8,128)S(1)}, f32[2,160,2048]{2,1,0:T(8,128)}, u32[]{:S(2)}) copy-start(f32[2,160,2048]{2,1,0:T(8,128)} %param.6) | copy-start | bytes 7864324
  506.8 264.1 %all-gather.10.cloned.1.call-start = ((), (), s32[]{:S(2)}) async-start(), calls=%async_computation.6 | async-start | bytes 6553600 | tf_op jit(solution)/reshape | solution.py:52
  770.9 6.2 copy-start.2
  770.9 8.5 %slice-start.2 = ((s8[5242880]{0:T(1024)(128)(4,1)}), s8[4194304]{0:T(1024)(128)(4,1)S(1)}, s32[]{:S(2)}) async-start(s8[5242880]{0:T(1024)(128)(4,1)} %bitcast.362), calls=%async_computation.17 | async-start | bytes 8388608
  777.1 2.4 slice-start.3
  (2 other events, 1.3 us)
Sparse Core Ops, SparseCore 0:
  284.8 54.2 reduce-scatter.28
  341.3 51.0 reduce-scatter.26
  394.7 51.0 reduce-scatter.24
  447.9 51.0 reduce-scatter.22
  501.7 51.0 reduce-scatter.18
  555.5 51.0 reduce-scatter.20
  608.1 52.4 all-gather.13
  662.1 53.2 all-gather.11
  717.6 53.2 all-gather.9
where the time goes:
time: 797 us; the launch traced here: 789 us
  matrix products  333 us (42%)
  waiting for transfers between devices  308 us (39%)
  other arithmetic  97.7 us (12%)
  local copies, waits for them, and re-layouts  34.8 us (4%)
  between operations  14.9 us (2%)
    reshape x3, waiting for transfers between devices, step(): t.reshape(-1, *t.shape[2:])  157 us
    unnamed x15, waiting for transfers between devices  151 us
    dot_general x5, matrix products, layer(): gate = jnp.dot(a, w['w_gate'], preferred_element_type=jnp.float32)  117 us
    dot_general x5, matrix products, layer(): up = jnp.dot(a, w['w_up'], preferred_element_type=jnp.float32)  111 us
    dot_general x5, matrix products, matmul(): jnp.dot(a, w, preferred_element_type=jnp.float32).astype(jnp.bfloat16)  105 us
    unnamed x5, other arithmetic  66.6 us
    unnamed x39, local copies, waits for them, and re-layouts  34.2 us
    reshape x3, other arithmetic, step(): t.reshape(-1, *t.shape[2:])  19 us
  transfers between devices with their start and end apart: 9, of which 7 were waited for; matrix products, arithmetic and copies ran while one was open for 22% of the time, Pallas kernels for 0%

commit v1 on v0

v1 whole, which is shorter than its diff:
```python
import functools

import jax
import jax.numpy as jnp
from jax import lax
from jax.experimental import pallas as pl
from jax.experimental.pallas import tpu as pltpu
from jax.sharding import PartitionSpec as P

F32, BF16 = jnp.float32, jnp.bfloat16
TILE = 512
LANES = 128


def nn(a, b):
    return lax.dot_general(a, b, (((1,), (0,)), ((), ())), preferred_element_type=F32)


def nt(a, b):
    return lax.dot_general(a, b, (((1,), (1,)), ((), ())), preferred_element_type=F32)


def tn(a, b):
    return lax.dot_general(a, b, (((0,), (0,)), ((), ())), preferred_element_type=F32)


def normed(h):
    wide = h.astype(F32)
    scale = lax.rsqrt(jnp.mean(wide * wide, -1, keepdims=True) + 1e-6)
    return (wide * scale).astype(BF16)


def normed_back(h, by_a):
    wide = h.astype(F32)
    scale = lax.rsqrt(jnp.mean(wide * wide, -1, keepdims=True) + 1e-6)
    along = jnp.mean(by_a * wide, -1, keepdims=True)
    return (scale * by_a - wide * (scale * scale * scale * along)).astype(BF16)


def kernel(
    n,
    x_in, dy_in, wg_in, wu_in, wd_in, mg_in, mu_in, md_in, vg_in, vu_in, vd_in,
    wg_out, wu_out, wd_out, mg_out, mu_out, md_out, vg_out, vu_out, vd_out,
    x, h1, dy, a, acc, accgu, accd, wg, wu, wd,
    s1gu, s1d, r1gu, r1d, s2gu, s2d, r2gu, r2d, wngu, wnd, mvgu, mvd,
    tile_sem, w_sem, ld_sem, st_sem,
    rs1_send, rs1_recv, rs2_send, rs2_recv, ag1_send, ag1_recv, ag2_send, ag2_recv,
):
    tokens, d_model = x.shape
    ff = wg_in.shape[2]
    tiles = tokens // TILE
    share = ff // n
    chunks = share // LANES
    chunk = n * LANES
    rows = d_model // n
    half = LANES // 2

    me = lax.axis_index("dp")
    right, left, far = (lax.rem(me + k, n) for k in (1, n - 1, n // 2))

    def cols_of(owner, i):
        return pl.ds(pl.multiple_of(owner * share + i * LANES, LANES), LANES)

    def rows_of(owner):
        return pl.ds(pl.multiple_of(owner * rows, rows), rows)

    def units_of(owner):
        return pl.ds(pl.multiple_of(owner * LANES, LANES), LANES)

    def same(ref, sem):
        return pltpu.make_async_copy(ref, ref, sem)

    def part(owner):
        return slice(owner * LANES, (owner + 1) * LANES)

    def load_w(k):
        slot, layer, i = k % 2, (k // chunks) % 2, k % chunks
        for o in range(n):
            pltpu.make_async_copy(wg_in.at[layer, :, cols_of(o, i)], wg.at[slot, :, part(o)], w_sem.at[slot, 0]).start()
            pltpu.make_async_copy(wu_in.at[layer, :, cols_of(o, i)], wu.at[slot, :, part(o)], w_sem.at[slot, 1]).start()
            pltpu.make_async_copy(wd_in.at[layer, cols_of(o, i), :], wd.at[slot, part(o), :], w_sem.at[slot, 2]).start()

    def wait_w(k):
        slot = k % 2
        for j, ref in enumerate((wg, wu, wd)):
            same(ref.at[slot], w_sem.at[slot, j]).wait()

    def where(c):
        return c % 2, 1 - c // chunks, c % chunks

    def load_mvw(c):
        s, layer, i = where(c)
        for j, (m_in, v_in, w_in) in enumerate(((mg_in, vg_in, wg_in), (mu_in, vu_in, wu_in))):
            for o in range(n):
                pltpu.make_async_copy(m_in.at[layer, :, cols_of(o, i)], mvgu.at[s, 0, j, :, part(o)], ld_sem.at[s, 0]).start()
                pltpu.make_async_copy(v_in.at[layer, :, cols_of(o, i)], mvgu.at[s, 1, j, :, part(o)], ld_sem.at[s, 0]).start()
                pltpu.make_async_copy(w_in.at[layer, rows_of(me), cols_of(o, i)], wngu.at[s, j, :, part(o)], ld_sem.at[s, 2]).start()
        mine = pl.ds(pl.multiple_of(i * LANES, LANES), LANES)
        pltpu.make_async_copy(md_in.at[layer, mine, :], mvd.at[s, 0], ld_sem.at[s, 1]).start()
        pltpu.make_async_copy(vd_in.at[layer, mine, :], mvd.at[s, 1], ld_sem.at[s, 1]).start()
        pltpu.make_async_copy(wd_in.at[layer, cols_of(me, i), :], wnd.at[s], ld_sem.at[s, 3]).start()

    def wait_four(c, sem):
        s = c % 2
        for j, ref in enumerate((mvgu, mvd, wngu, wnd)):
            same(ref.at[s], sem.at[s, j]).wait()

    def store_mvw(c):
        s, layer, i = where(c)
        for j, (m_out, v_out, w_out) in enumerate(((mg_out, vg_out, wg_out), (mu_out, vu_out, wu_out))):
            for o in range(n):
                pltpu.make_async_copy(mvgu.at[s, 0, j, :, part(o)], m_out.at[layer, :, cols_of(o, i)], st_sem.at[s, 0]).start()
                pltpu.make_async_copy(mvgu.at[s, 1, j, :, part(o)], v_out.at[layer, :, cols_of(o, i)], st_sem.at[s, 0]).start()
                pltpu.make_async_copy(wngu.at[s, j, :, part(o)], w_out.at[layer, rows_of(me), cols_of(o, i)], st_sem.at[s, 2]).start()
        mine = pl.ds(pl.multiple_of(i * LANES, LANES), LANES)
        pltpu.make_async_copy(mvd.at[s, 0], md_out.at[layer, mine, :], st_sem.at[s, 1]).start()
        pltpu.make_async_copy(mvd.at[s, 1], vd_out.at[layer, mine, :], st_sem.at[s, 1]).start()
        pltpu.make_async_copy(wnd.at[s], wd_out.at[layer, cols_of(me, i), :], st_sem.at[s, 3]).start()

    def send(src, dst, send_sem, recv_sem, to):
        pltpu.make_async_remote_copy(
            src_ref=src, dst_ref=dst, send_sem=send_sem, recv_sem=recv_sem,
            device_id={"dp": to}, device_id_type=pl.DeviceIdType.MESH,
        ).start()

    def sum_1(c):
        s = c % 2
        for j, to in enumerate((right, left)):
            s1gu[j] = accgu[s, j, rows_of(far), :].astype(BF16)
        down = accd[s, :, units_of(far)].T
        s1d[0] = down[:half].astype(BF16)
        s1d[1] = down[half:].astype(BF16)
        for j, to in enumerate((right, left)):
            send(s1gu.at[j], r1gu.at[s, j], rs1_send.at[j, 0], rs1_recv.at[s, j, 0], to)
            send(s1d.at[j], r1d.at[s, j], rs1_send.at[j, 1], rs1_recv.at[s, j, 1], to)

    def sum_2(c):
        s = c % 2
        for j, to in enumerate((right, left)):
            same(s1gu.at[j], rs1_send.at[j, 0]).wait()
            same(s1d.at[j], rs1_send.at[j, 1]).wait()
            same(r1gu.at[s, j], rs1_recv.at[s, j, 0]).wait()
            same(r1d.at[s, j], rs1_recv.at[s, j, 1]).wait()
            for k in range(2):
                total = accgu[s, k, rows_of(to), :]
                if k == j:
                    total += r1gu[s, j].astype(F32)
                s2gu[j, k] = total.astype(BF16)
            down = accd[s, :, units_of(to)].T
            for k in range(2):
                total = down[k * half : (k + 1) * half]
                if k == j:
                    total += r1d[s, j].astype(F32)
                s2d[j, k * half : (k + 1) * half] = total.astype(BF16)
            send(s2gu.at[j], r2gu.at[s, j], rs2_send.at[j, 0], rs2_recv.at[s, j, 0], to)
            send(s2d.at[j], r2d.at[s, j], rs2_send.at[j, 1], rs2_recv.at[s, j, 1], to)

    def adamw(w, m, v, g):
        g = g.astype(BF16).astype(F32)
        m = 0.9 * m + 0.1 * g
        v = 0.95 * v + 0.05 * g * g
        w = w.astype(F32)
        return (w - 0.02 * (m * lax.rsqrt(v + 1e-8) + 0.1 * w)).astype(BF16), m, v

    def sum_3(c):
        s, layer, i = where(c)
        for j in range(2):
            same(s2gu.at[j], rs2_send.at[j, 0]).wait()
            same(s2d.at[j], rs2_send.at[j, 1]).wait()
            same(r2gu.at[s, j], rs2_recv.at[s, j, 0]).wait()
            same(r2d.at[s, j], rs2_recv.at[s, j, 1]).wait()
        wait_four(c, ld_sem)
        for k in range(2):
            g = accgu[s, k, rows_of(me), :] + r2gu[s, 0, k].astype(F32) + r2gu[s, 1, k].astype(F32)
            wngu[s, k], mvgu[s, 0, k], mvgu[s, 1, k] = adamw(wngu[s, k], mvgu[s, 0, k], mvgu[s, 1, k], g)
        g = accd[s, :, units_of(me)].T + r2d[s, 0].astype(F32) + r2d[s, 1].astype(F32)
        wnd[s], mvd[s, 0], mvd[s, 1] = adamw(wnd[s], mvd[s, 0], mvd[s, 1], g)
        for j, to in enumerate((right, left)):
            for k, w_out in enumerate((wg_out, wu_out)):
                for o in range(n):
                    send(wngu.at[s, k, :, part(o)], w_out.at[layer, rows_of(me), cols_of(o, i)],
                         ag1_send.at[s, j, 0], ag1_recv.at[s, j, 0], to)
            send(wnd.at[s], wd_out.at[layer, cols_of(me, i), :], ag1_send.at[s, j, 1], ag1_recv.at[s, j, 1], to)
        store_mvw(c)

    def gather_2(c):
        s, layer, i = where(c)
        for j, (w_out, owner, to) in enumerate(((wg_out, left, right), (wu_out, right, left))):
            same(wngu.at[s], ag1_recv.at[s, j, 0]).wait()
            same(wnd.at[s], ag1_recv.at[s, j, 1]).wait()
            for o in range(n):
                block = w_out.at[layer, rows_of(owner), cols_of(o, i)]
                send(block, block, ag2_send.at[s, j, 0], ag2_recv.at[s, j, 0], to)
            block = wd_out.at[layer, pl.ds(pl.multiple_of(owner * share + i * LANES + j * half, half), half), :]
            send(block, block, ag2_send.at[s, j, 1], ag2_recv.at[s, j, 1], to)

    def finish(c):
        s = c % 2
        for j in range(2):
            same(wngu.at[s], ag1_send.at[s, j, 0]).wait()
            same(wnd.at[s], ag1_send.at[s, j, 1]).wait()
            for sems in (ag2_send, ag2_recv):
                same(wngu.at[s, 0], sems.at[s, j, 0]).wait()
                same(wnd.at[s, :half], sems.at[s, j, 1]).wait()
        wait_four(c, st_sem)

    def rows_at(t):
        return pl.ds(pl.multiple_of(t * TILE, TILE), TILE)

    def copy_x(t):
        return pltpu.make_async_copy(x_in.at[0, rows_at(t)], x.at[rows_at(t)], tile_sem.at[0, t])

    def copy_dy(t):
        return pltpu.make_async_copy(dy_in.at[0, rows_at(t)], dy.at[rows_at(t)], tile_sem.at[1, t])

    load_w(0)
    for t in range(tiles):
        copy_x(t).start()
    for t in range(tiles):
        copy_dy(t).start()

    barrier = pltpu.get_barrier_semaphore()
    for to in (left, right):
        pl.semaphore_signal(barrier, inc=1, device_id={"dp": to}, device_id_type=pl.DeviceIdType.MESH)
    pl.semaphore_wait(barrier, 2)

    def begin(k):
        wait_w(k)

        @pl.when(k + 1 < 3 * chunks)
        def _():
            load_w(k + 1)

    @pl.loop(0, chunks)
    def _(i):
        begin(i)
        slot = i % 2

        @pl.loop(0, tiles)
        def _(t):
            r = rows_at(t)

            @pl.when(i == 0)
            def _():
                copy_x(t).wait()
                a[r] = normed(x[r])
                acc[r] = jnp.zeros((TILE, d_model), F32)

            at = a[r]
            gate, up = nn(at, wg[slot]), nn(at, wu[slot])
            hidden = (gate * jax.nn.sigmoid(gate) * up).astype(BF16)
            acc[r] += nn(hidden, wd[slot])

            @pl.when(i == chunks - 1)
            def _():
                h1[r] = x[r] + acc[r].astype(BF16)

    def backward(k, i, states, last):
        c = k - chunks
        s, slot = c % 2, k % 2
        begin(k)

        @pl.loop(0, tiles)
        def _(t):
            r = rows_at(t)

            @pl.when(i == 0)
            def _():
                if last:
                    copy_dy(t).wait()
                    acc[r] = jnp.zeros((TILE, d_model), F32)
                a[r] = normed(states[r])

            at, dyt = a[r], dy[r]
            gate, up = nn(at, wg[slot]), nn(at, wu[slot])
            by_hidden = nt(dyt, wd[slot]).astype(BF16).astype(F32)
            sigmoid = jax.nn.sigmoid(gate)
            silu = gate * sigmoid
            hidden = (silu * up).astype(BF16)
            by_up = (by_hidden * silu).astype(BF16)
            by_gate = (by_hidden * up * (sigmoid + silu * (1 - sigmoid))).astype(BF16)
            new = t == 0
            accd[s] = jnp.where(new, 0.0, accd[s]) + tn(dyt, hidden)
            accgu[s, 0] = jnp.where(new, 0.0, accgu[s, 0]) + tn(at, by_gate)
            accgu[s, 1] = jnp.where(new, 0.0, accgu[s, 1]) + tn(at, by_up)
            if last:
                acc[r] += nt(by_gate, wg[slot]) + nt(by_up, wu[slot])

                @pl.when(i == chunks - 1)
                def _():
                    dy[r] = dyt + normed_back(states[r], acc[r].astype(BF16).astype(F32))

            @pl.when((t == tiles * 3 // 8) & (c >= 2))
            def _():
                gather_2(c - 2)

            @pl.when((t == tiles * 5 // 8) & (c >= 1))
            def _():
                sum_2(c - 1)

        sum_1(c)

        @pl.when(c >= 2)
        def _():
            finish(c - 2)

        load_mvw(c)

        @pl.when(c >= 1)
        def _():
            sum_3(c - 1)

    @pl.loop(0, chunks)
    def _(i):
        backward(chunks + i, i, h1, True)

    @pl.loop(0, chunks)
    def _(i):
        backward(2 * chunks + i, i, x, False)

    end = 2 * chunks - 1
    sum_2(end)
    gather_2(end - 1)
    sum_3(end)
    finish(end - 1)
    gather_2(end)
    finish(end)


def solution(mesh):
    n = mesh.shape["dp"]

    def step(x, dy, *arrays):
        weights, moments = arrays[:3], arrays[3:]
        tokens, d_model = x.shape[1:]
        ff = weights[0].shape[2]
        chunk, rows, half = n * LANES, d_model // n, LANES // 2
        out = lambda like, dtype: jax.ShapeDtypeStruct(like.shape, dtype)
        vmem, dma = pltpu.VMEM, pltpu.SemaphoreType.DMA
        return pl.pallas_call(
            functools.partial(kernel, n),
            out_shape=[out(w, BF16) for w in weights] + [out(m, F32) for m in moments],
            in_specs=[pl.BlockSpec(memory_space=pl.ANY)] * 11,
            out_specs=[pl.BlockSpec(memory_space=pl.ANY)] * 9,
            scratch_shapes=[
                vmem((tokens, d_model), BF16),
                vmem((tokens, d_model), BF16),
                vmem((tokens, d_model), BF16),
                vmem((tokens, d_model), BF16),
                vmem((tokens, d_model), F32),
                vmem((2, 2, d_model, chunk), F32),
                vmem((2, d_model, chunk), F32),
                vmem((2, d_model, chunk), BF16),
                vmem((2, d_model, chunk), BF16),
                vmem((2, chunk, d_model), BF16),
                vmem((2, rows, chunk), BF16),
                vmem((2, half, d_model), BF16),
                vmem((2, 2, rows, chunk), BF16),
                vmem((2, 2, half, d_model), BF16),
                vmem((2, 2, rows, chunk), BF16),
                vmem((2, LANES, d_model), BF16),
                vmem((2, 2, 2, rows, chunk), BF16),
                vmem((2, 2, LANES, d_model), BF16),
                vmem((2, 2, rows, chunk), BF16),
                vmem((2, LANES, d_model), BF16),
                vmem((2, 2, 2, rows, chunk), F32),
                vmem((2, 2, LANES, d_model), F32),
                dma((2, tokens // TILE)),
                dma((2, 3)),
                dma((2, 4)),
                dma((2, 4)),
                dma((2, 2)),
                dma((2, 2, 2)),
                dma((2, 2)),
                dma((2, 2, 2)),
                dma((2, 2, 2)),
                dma((2, 2, 2)),
                dma((2, 2, 2)),
                dma((2, 2, 2)),
            ],
            compiler_params=pltpu.CompilerParams(
                collective_id=0, has_side_effects=True, vmem_limit_bytes=67043328
            ),
            name="train_step",
        )(x, dy, *arrays)

    tokens, whole = P(("rep", "dp"), None, None), P(None, None, None)
    shares = [P(None, "dp", None)] * 6
    return jax.shard_map(
        step,
        mesh=mesh,
        in_specs=(tokens, tokens, whole, whole, whole, *shares),
        out_specs=tuple([P("rep", None, None)] * 3 + [P("rep", "dp", None)] * 6),
        check_vma=False,
    )
```

time: 797 us -> 405 us (0.51); the launches traced: 789 us -> 405 us
  Pallas kernels: 0 us -> 377 us
  matrix products: 333 us -> 0 us
  waiting for transfers between devices: 308 us -> 0 us
  other arithmetic: 97.7 us -> 0.01 us
  between operations: 14.9 us -> 0.69 us
    pallas_call x0 -> x1, Pallas kernels: none -> 377 us  [step(): pl.pallas_call(functools.partial(kernel, n), out_shape=[out(w, BF16) for...]
    dot_general x15 -> x0, matrix products: 333 us -> none  [the longest x5 117 us: layer(): gate = jnp.dot(a, w['w_gate'], preferred_element_type=jnp.float32)]
    reshape x3 -> x0, waiting for transfers between devices: 157 us -> none  [step(): t.reshape(-1, *t.shape[2:])]
    unnamed x15 -> x0, waiting for transfers between devices: 151 us -> none
    unnamed x5 -> x1, other arithmetic: 66.6 us -> 0.01 us
    reshape x3 -> x0, other arithmetic: 19 us -> none  [step(): t.reshape(-1, *t.shape[2:])]
    broadcast_in_dim x6 -> x0, other arithmetic: 8.43 us -> none  [stack(): h = layer(h, {name: w[number] for name, w in weights.items()})]
    unnamed x39 -> x27, local copies, waits for them, and re-layouts: 34.2 us -> 27.1 us
  transfers between devices with their start and end apart: 9 -> 0, of which waited for: 7 -> 0; matrix products, arithmetic and copies ran while one was open for 22% -> 0% of each run, Pallas kernels for 0% -> 0%
where the time goes in v1:
time: 405 us
  Pallas kernels  377 us (93%)
  local copies, waits for them, and re-layouts  27.1 us (7%)
    pallas_call x1, Pallas kernels, step(): pl.pallas_call(functools.partial(kernel, n), out_shape=[out(w, BF16) for...  377 us
    unnamed x27, local copies, waits for them, and re-layouts  27.1 us

profile of v1, /device:TPU:112, one launch (start us, length us, event | category | flops | bytes accessed | tf_op | source)
XLA Modules:
  0.0 404.7 jit_solution(2884754610182591056)
XLA Ops:
  0.6 376.9 %train_step.1 = (bf16[2,640,2048]{2,1,0:T(8,128)(2,1)}, bf16[2,640,2048]{2,1,0:T(8,128)(2,1)}, bf16[2,2048,640]{2,1,0:T(8,128)(2,1)}, f32[2,160,2048]{2,1,0:T(8,...) custom-call(bf16[1,4096,640]{2,1,0:T(8,128)(2,1)} %x_in.1, ...), custom_call_target="tpu_custom_call" | custom-call | tf_op jit(solution)/shard_map/train_step/pallas_call | solution.py:340
  377.6 0.0 copy-start
  377.6 0.0 slice-start
  377.6 6.2 %copy.29 = bf16[2,640,2048]{2,1,0:T(8,128)(2,1)} copy(bf16[2,640,2048]{2,1,0:T(8,128)(2,1)} %get-tuple-element.18) | data formatting | bytes 10485760
  383.8 0.0 copy-done
  383.8 0.0 slice-start.1
  383.8 2.4 copy.30
  386.1 0.0 slice-done
  386.1 0.0 slice-done.1
  386.1 2.7 copy.31
  388.8 1.0 copy-done.6
  389.8 0.0 copy-start.5
  389.8 1.5 copy.32
  391.3 1.2 copy-done.5
  392.5 0.0 copy-start.4
  392.5 1.5 copy.33
  393.9 1.2 copy-done.4
  395.1 1.5 copy.34
  396.6 1.2 copy-done.3
  397.8 1.5 copy.35
  399.3 1.2 copy-done.2
  400.5 1.5 copy.36
  402.0 1.2 copy-done.1
  403.2 1.5 copy.37
  (5 shorter events, 0.0 us)
Async XLA Ops:
  377.6 6.2 %copy-start = (bf16[2,640,2048]{2,1,0:T(8,128)(2,1)S(1)}, bf16[2,640,2048]{2,1,0:T(8,128)(2,1)}, u32[]{:S(2)}) copy-start(bf16[2,640,2048]{2,1,0:T(8,128)(2,1)} %get-tuple-element.19) | copy-start | bytes 15728644
  377.6 8.5 %slice-start = ((s8[5242880]{0:T(1024)(128)(4,1)}), s8[4194304]{0:T(1024)(128)(4,1)S(1)}, s32[]{:S(2)}) async-start(s8[5242880]{0:T(1024)(128)(4,1)} %bitcast), calls=%async_computation | async-start | bytes 8388608
  383.8 2.4 slice-start.1
  386.1 3.6 copy-start.6
  389.8 2.7 copy-start.5
  392.5 2.7 copy-start.4
  395.1 2.7 copy-start.3
  397.8 2.7 copy-start.2
  400.5 2.7 copy-start.1

commit v2 on v1

v2 whole, which is shorter than its diff:
```python
import functools

import jax
import jax.numpy as jnp
from jax import lax
from jax.experimental import pallas as pl
from jax.experimental.pallas import tpu as pltpu
from jax.sharding import PartitionSpec as P

F32, BF16 = jnp.float32, jnp.bfloat16
TILE = 1024
LANES = 128
HALVES = 2


def nn(a, b):
    return lax.dot_general(a, b, (((1,), (0,)), ((), ())), preferred_element_type=F32)


def nt(a, b):
    return lax.dot_general(a, b, (((1,), (1,)), ((), ())), preferred_element_type=F32)


def tn(a, b):
    return lax.dot_general(a, b, (((0,), (0,)), ((), ())), preferred_element_type=F32)


def normed(h):
    wide = h.astype(F32)
    scale = lax.rsqrt(jnp.mean(wide * wide, -1, keepdims=True) + 1e-6)
    return (wide * scale).astype(BF16)


def normed_back(h, by_a):
    wide = h.astype(F32)
    scale = lax.rsqrt(jnp.mean(wide * wide, -1, keepdims=True) + 1e-6)
    along = jnp.mean(by_a * wide, -1, keepdims=True)
    return (scale * by_a - wide * (scale * scale * scale * along)).astype(BF16)


def kernel(
    n,
    x_in, dy_in, wg_in, wu_in, wd_in, mg_in, mu_in, md_in, vg_in, vu_in, vd_in,
    wg_out, wu_out, wd_out, mg_out, mu_out, md_out, vg_out, vu_out, vd_out,
    x, h1, dy, a, acc, accgu, accd, wg, wu, wd,
    s1gu, s1d, r1gu, r1d, s2gu, s2d, r2gu, r2d, wngu, wnd, mvgu, mvd,
    tile_sem, w_sem, ld_sem, st_sem,
    rs1_send, rs1_recv, rs2_send, rs2_recv, ag1_send, ag1_recv, ag2_send, ag2_recv,
):
    tokens, d_model = x.shape
    ff = wg_in.shape[2]
    tiles = tokens // TILE
    share = ff // n
    chunks = share // LANES
    owners = n // HALVES
    width = owners * LANES
    units = chunks * HALVES
    rows = d_model // n
    half = LANES // 2

    me = lax.axis_index("dp")
    right, left, far = (lax.rem(me + k, n) for k in (1, n - 1, n // 2))

    def cols_of(owner, i):
        return pl.ds(pl.multiple_of(owner * share + i * LANES, LANES), LANES)

    def rows_of(owner):
        return pl.ds(pl.multiple_of(owner * rows, rows), rows)

    def units_of(owner):
        return pl.ds(pl.multiple_of(owner * LANES, LANES), LANES)

    def same(ref, sem):
        return pltpu.make_async_copy(ref, ref, sem)

    def part(owner):
        return slice(owner * LANES, (owner + 1) * LANES)

    def load_w(k):
        slot, layer, i = k % 2, (k // chunks) % 2, k % chunks
        for o in range(n):
            pltpu.make_async_copy(wg_in.at[layer, :, cols_of(o, i)], wg.at[slot, :, part(o)], w_sem.at[slot, 0]).start()
            pltpu.make_async_copy(wu_in.at[layer, :, cols_of(o, i)], wu.at[slot, :, part(o)], w_sem.at[slot, 1]).start()
            pltpu.make_async_copy(wd_in.at[layer, cols_of(o, i), :], wd.at[slot, part(o), :], w_sem.at[slot, 2]).start()

    def wait_w(k):
        slot = k % 2
        for j, ref in enumerate((wg, wu, wd)):
            same(ref.at[slot], w_sem.at[slot, j]).wait()

    def where(u):
        return u % HALVES, 1 - u // units, (u // HALVES) % chunks

    def second(h, do):
        pl.when(h == HALVES - 1)(do)

    def load_mvw(u):
        h, layer, i = where(u)
        for q in range(owners):
            cols = cols_of(h * owners + q, i)
            for j, (m_in, v_in, w_in) in enumerate(((mg_in, vg_in, wg_in), (mu_in, vu_in, wu_in))):
                pltpu.make_async_copy(m_in.at[layer, :, cols], mvgu.at[h, 0, j, :, part(q)], ld_sem.at[h, 0]).start()
                pltpu.make_async_copy(v_in.at[layer, :, cols], mvgu.at[h, 1, j, :, part(q)], ld_sem.at[h, 0]).start()
                pltpu.make_async_copy(w_in.at[layer, rows_of(me), cols], wngu.at[h, j, :, part(q)], ld_sem.at[h, 1]).start()

        def down():
            mine = pl.ds(pl.multiple_of(i * LANES, LANES), LANES)
            pltpu.make_async_copy(md_in.at[layer, mine, :], mvd.at[0], ld_sem.at[0, 2]).start()
            pltpu.make_async_copy(vd_in.at[layer, mine, :], mvd.at[1], ld_sem.at[0, 2]).start()
            pltpu.make_async_copy(wd_in.at[layer, cols_of(me, i), :], wnd, ld_sem.at[1, 2]).start()

        second(h, down)

    def wait_mvw(u, sem):
        h = u % HALVES
        same(mvgu.at[h], sem.at[h, 0]).wait()
        same(wngu.at[h], sem.at[h, 1]).wait()

        def down():
            same(mvd, sem.at[0, 2]).wait()
            same(wnd, sem.at[1, 2]).wait()

        second(h, down)

    def store_mvw(u):
        h, layer, i = where(u)
        for q in range(owners):
            cols = cols_of(h * owners + q, i)
            for j, (m_out, v_out, w_out) in enumerate(((mg_out, vg_out, wg_out), (mu_out, vu_out, wu_out))):
                pltpu.make_async_copy(mvgu.at[h, 0, j, :, part(q)], m_out.at[layer, :, cols], st_sem.at[h, 0]).start()
                pltpu.make_async_copy(mvgu.at[h, 1, j, :, part(q)], v_out.at[layer, :, cols], st_sem.at[h, 0]).start()
                pltpu.make_async_copy(wngu.at[h, j, :, part(q)], w_out.at[layer, rows_of(me), cols], st_sem.at[h, 1]).start()

        def down():
            mine = pl.ds(pl.multiple_of(i * LANES, LANES), LANES)
            pltpu.make_async_copy(mvd.at[0], md_out.at[layer, mine, :], st_sem.at[0, 2]).start()
            pltpu.make_async_copy(mvd.at[1], vd_out.at[layer, mine, :], st_sem.at[0, 2]).start()
            pltpu.make_async_copy(wnd, wd_out.at[layer, cols_of(me, i), :], st_sem.at[1, 2]).start()

        second(h, down)

    def send(src, dst, send_sem, recv_sem, to):
        pltpu.make_async_remote_copy(
            src_ref=src, dst_ref=dst, send_sem=send_sem, recv_sem=recv_sem,
            device_id={"dp": to}, device_id_type=pl.DeviceIdType.MESH,
        ).start()

    def sum_1(u):
        h, _, i = where(u)
        for j, to in enumerate((right, left)):
            s1gu[j] = accgu[h, j, rows_of(far), :].astype(BF16)
            send(s1gu.at[j], r1gu.at[h, j], rs1_send.at[j, 0], rs1_recv.at[h, j], to)

        def down():
            block = accd[i % 2, :, units_of(far)].T
            for j, to in enumerate((right, left)):
                s1d[j] = block[j * half : (j + 1) * half].astype(BF16)
                send(s1d.at[j], r1d.at[j], rs1_send.at[j, 1], rs1_recv.at[2, j], to)

        second(h, down)

    def sum_2(u):
        h, _, i = where(u)
        for j, to in enumerate((right, left)):
            same(s1gu.at[j], rs1_send.at[j, 0]).wait()
            same(r1gu.at[h, j], rs1_recv.at[h, j]).wait()
            for k in range(2):
                total = accgu[h, k, rows_of(to), :]
                if k == j:
                    total += r1gu[h, j].astype(F32)
                s2gu[j, k] = total.astype(BF16)
            send(s2gu.at[j], r2gu.at[h, j], rs2_send.at[j, 0], rs2_recv.at[h, j], to)

        def down():
            for j, to in enumerate((right, left)):
                same(s1d.at[j], rs1_send.at[j, 1]).wait()
                same(r1d.at[j], rs1_recv.at[2, j]).wait()
                block = accd[i % 2, :, units_of(to)].T
                for k in range(2):
                    total = block[k * half : (k + 1) * half]
                    if k == j:
                        total += r1d[j].astype(F32)
                    s2d[j, k * half : (k + 1) * half] = total.astype(BF16)
                send(s2d.at[j], r2d.at[j], rs2_send.at[j, 1], rs2_recv.at[2, j], to)

        second(h, down)

    def adamw(w, m, v, g):
        g = g.astype(BF16).astype(F32)
        m = 0.9 * m + 0.1 * g
        v = 0.95 * v + 0.05 * g * g
        w = w.astype(F32)
        return (w - 0.02 * (m * lax.rsqrt(v + 1e-8) + 0.1 * w)).astype(BF16), m, v

    def sum_3(u):
        h, layer, i = where(u)
        wait_mvw(u, ld_sem)
        for j in range(2):
            same(s2gu.at[j], rs2_send.at[j, 0]).wait()
            same(r2gu.at[h, j], rs2_recv.at[h, j]).wait()
        for k in range(2):
            g = accgu[h, k, rows_of(me), :] + r2gu[h, 0, k].astype(F32) + r2gu[h, 1, k].astype(F32)
            wngu[h, k], mvgu[h, 0, k], mvgu[h, 1, k] = adamw(wngu[h, k], mvgu[h, 0, k], mvgu[h, 1, k], g)
        for j, to in enumerate((right, left)):
            for k, w_out in enumerate((wg_out, wu_out)):
                for q in range(owners):
                    send(wngu.at[h, k, :, part(q)], w_out.at[layer, rows_of(me), cols_of(h * owners + q, i)],
                         ag1_send.at[h, j], ag1_recv.at[h, j], to)

        def down():
            for j in range(2):
                same(s2d.at[j], rs2_send.at[j, 1]).wait()
                same(r2d.at[j], rs2_recv.at[2, j]).wait()
            g = accd[i % 2, :, units_of(me)].T + r2d[0].astype(F32) + r2d[1].astype(F32)
            wnd[...], mvd[0], mvd[1] = adamw(wnd[...], mvd[0], mvd[1], g)
            for j, to in enumerate((right, left)):
                send(wnd, wd_out.at[layer, cols_of(me, i), :], ag1_send.at[2, j], ag1_recv.at[2, j], to)

        second(h, down)
        store_mvw(u)

    def gather_2(u):
        h, layer, i = where(u)
        ways = tuple(enumerate(((wg_out, left, right), (wu_out, right, left))))
        for j, (w_out, owner, to) in ways:
            same(wngu.at[h], ag1_recv.at[h, j]).wait()
            for q in range(owners):
                block = w_out.at[layer, rows_of(owner), cols_of(h * owners + q, i)]
                send(block, block, ag2_send.at[h, j], ag2_recv.at[h, j], to)

        def down():
            for j, (_, owner, to) in ways:
                same(wnd, ag1_recv.at[2, j]).wait()
                block = wd_out.at[layer, pl.ds(pl.multiple_of(owner * share + i * LANES + j * half, half), half), :]
                send(block, block, ag2_send.at[2, j], ag2_recv.at[2, j], to)

        second(h, down)

    def finish(u):
        h = u % HALVES
        for j in range(2):
            same(wngu.at[h], ag1_send.at[h, j]).wait()
            for sems in (ag2_send, ag2_recv):
                same(wngu.at[h, 0], sems.at[h, j]).wait()

        def down():
            for j in range(2):
                same(wnd, ag1_send.at[2, j]).wait()
                for sems in (ag2_send, ag2_recv):
                    same(wnd.at[:half], sems.at[2, j]).wait()

        second(h, down)
        wait_mvw(u, st_sem)

    def rows_at(t):
        return pl.ds(pl.multiple_of(t * TILE, TILE), TILE)

    def copy_x(t):
        return pltpu.make_async_copy(x_in.at[0, rows_at(t)], x.at[rows_at(t)], tile_sem.at[0, t])

    def copy_dy(t):
        return pltpu.make_async_copy(dy_in.at[0, rows_at(t)], dy.at[rows_at(t)], tile_sem.at[1, t])

    load_w(0)
    for t in range(tiles):
        copy_x(t).start()
    for t in range(tiles):
        copy_dy(t).start()

    barrier = pltpu.get_barrier_semaphore()
    for to in (left, right):
        pl.semaphore_signal(barrier, inc=1, device_id={"dp": to}, device_id_type=pl.DeviceIdType.MESH)
    pl.semaphore_wait(barrier, 2)

    def begin(k):
        wait_w(k)

        @pl.when(k + 1 < 3 * chunks)
        def _():
            load_w(k + 1)

    @pl.loop(0, chunks)
    def _(i):
        begin(i)
        slot = i % 2

        @pl.loop(0, tiles)
        def _(t):
            r = rows_at(t)

            @pl.when(i == 0)
            def _():
                copy_x(t).wait()
                a[r] = normed(x[r])
                acc[r] = jnp.zeros((TILE, d_model), F32)

            at = a[r]
            gate, up = nn(at, wg[slot]), nn(at, wu[slot])
            hidden = (gate * jax.nn.sigmoid(gate) * up).astype(BF16)
            acc[r] += nn(hidden, wd[slot])

            @pl.when(i == chunks - 1)
            def _():
                h1[r] = x[r] + acc[r].astype(BF16)

    def backward(u, states, last):
        h, _, i = where(u)
        k = chunks + u // HALVES
        slot = k % 2
        first = u % units == 0
        hidden_units = pl.ds(pl.multiple_of(h * width, width), width)

        @pl.when(h == 0)
        def _():
            begin(k)

        @pl.loop(0, tiles)
        def _(t):
            r = rows_at(t)

            @pl.when(first)
            def _():
                if last:
                    copy_dy(t).wait()
                    acc[r] = jnp.zeros((TILE, d_model), F32)
                a[r] = normed(states[r])

            at, dyt = a[r], dy[r]
            wgt, wut = wg[slot, :, hidden_units], wu[slot, :, hidden_units]
            gate, up = nn(at, wgt), nn(at, wut)
            by_hidden = nt(dyt, wd[slot, hidden_units, :]).astype(BF16).astype(F32)
            sigmoid = jax.nn.sigmoid(gate)
            silu = gate * sigmoid
            hidden = (silu * up).astype(BF16)
            by_up = (by_hidden * silu).astype(BF16)
            by_gate = (by_hidden * up * (sigmoid + silu * (1 - sigmoid))).astype(BF16)
            new = t == 0
            accd[i % 2, :, hidden_units] = jnp.where(new, 0.0, accd[i % 2, :, hidden_units]) + tn(dyt, hidden)
            accgu[h, 0] = jnp.where(new, 0.0, accgu[h, 0]) + tn(at, by_gate)
            accgu[h, 1] = jnp.where(new, 0.0, accgu[h, 1]) + tn(at, by_up)
            if last:
                acc[r] += nt(by_gate, wgt) + nt(by_up, wut)

                @pl.when(u == units - 1)
                def _():
                    dy[r] = dyt + normed_back(states[r], acc[r].astype(BF16).astype(F32))

            @pl.when(t == 0)
            def _():
                @pl.when(u >= 3)
                def _():
                    finish(u - 3)

                @pl.when(u >= 1)
                def _():
                    sum_2(u - 1)
                    load_mvw(u - 1)

            @pl.when((t == tiles - 2) & (u >= 2))
            def _():
                gather_2(u - 2)

        sum_1(u)

        @pl.when(u >= 1)
        def _():
            sum_3(u - 1)

    @pl.loop(0, units)
    def _(u):
        backward(u, h1, True)

    @pl.loop(units, 2 * units)
    def _(u):
        backward(u, x, False)

    end = 2 * units - 1
    finish(end - 2)
    sum_2(end)
    load_mvw(end)
    gather_2(end - 1)
    sum_3(end)
    finish(end - 1)
    gather_2(end)
    finish(end)


def pieces_of(shape, dtype):
    layers, height, width = shape
    cut = max(1, height * width * jnp.dtype(dtype).itemsize // 1300000)
    while height % (cut * 8):
        cut -= 1
    return [(l, slice(k * height // cut, (k + 1) * height // cut)) for l in range(layers) for k in range(cut)]


def copies(*refs):
    count = (len(refs) - 2) // 3
    source, target, held = (refs[k * count : (k + 1) * count] for k in range(3))
    in_sem, out_sem = refs[-2:]
    places = [(k, *at) for k, ref in enumerate(source) for at in pieces_of(ref.shape, ref.dtype)]
    way_in = [pltpu.make_async_copy(source[k].at[l, s], held[k].at[l, s], in_sem.at[p]) for p, (k, l, s) in enumerate(places)]
    way_out = [pltpu.make_async_copy(held[k].at[l, s], target[k].at[l, s], out_sem.at[p]) for p, (k, l, s) in enumerate(places)]
    for copy in way_in:
        copy.start()
    for p, copy in enumerate(way_out):
        way_in[p].wait()
        copy.start()
    for copy in way_out:
        copy.wait()


def solution(mesh):
    n = mesh.shape["dp"]
    most = 67043328

    def step(x, dy, *arrays):
        weights, moments = arrays[:3], arrays[3:]
        tokens, d_model = x.shape[1:]
        chunk, rows, half = n * LANES, d_model // n, LANES // 2
        width = chunk // HALVES
        shapes = [jax.ShapeDtypeStruct(w.shape, BF16) for w in weights] + [jax.ShapeDtypeStruct(m.shape, F32) for m in moments]
        vmem, dma = pltpu.VMEM, pltpu.SemaphoreType.DMA
        anywhere = pl.BlockSpec(memory_space=pl.ANY)
        new = pl.pallas_call(
            functools.partial(kernel, n),
            out_shape=shapes,
            in_specs=[anywhere] * 11,
            out_specs=[anywhere] * 9,
            scratch_shapes=[
                vmem((tokens, d_model), BF16),
                vmem((tokens, d_model), BF16),
                vmem((tokens, d_model), BF16),
                vmem((tokens, d_model), BF16),
                vmem((tokens, d_model), F32),
                vmem((HALVES, 2, d_model, width), F32),
                vmem((2, d_model, chunk), F32),
                vmem((2, d_model, chunk), BF16),
                vmem((2, d_model, chunk), BF16),
                vmem((2, chunk, d_model), BF16),
                vmem((2, rows, width), BF16),
                vmem((2, half, d_model), BF16),
                vmem((HALVES, 2, rows, width), BF16),
                vmem((2, half, d_model), BF16),
                vmem((2, 2, rows, width), BF16),
                vmem((2, LANES, d_model), BF16),
                vmem((HALVES, 2, 2, rows, width), BF16),
                vmem((2, LANES, d_model), BF16),
                vmem((HALVES, 2, rows, width), BF16),
                vmem((LANES, d_model), BF16),
                vmem((HALVES, 2, 2, rows, width), F32),
                vmem((2, LANES, d_model), F32),
                dma((2, tokens // TILE)),
                dma((2, 3)),
                dma((2, 3)),
                dma((2, 3)),
                dma((2, 2)),
                dma((HALVES + 1, 2)),
                dma((2, 2)),
                dma((HALVES + 1, 2)),
                dma((HALVES + 1, 2)),
                dma((HALVES + 1, 2)),
                dma((HALVES + 1, 2)),
                dma((HALVES + 1, 2)),
            ],
            compiler_params=pltpu.CompilerParams(collective_id=0, has_side_effects=True, vmem_limit_bytes=most),
            name="train_step",
        )(x, dy, *arrays)
        places = sum(len(pieces_of(s.shape, s.dtype)) for s in shapes)
        return pl.pallas_call(
            copies,
            out_shape=shapes,
            in_specs=[anywhere] * 9,
            out_specs=[anywhere] * 9,
            scratch_shapes=[vmem(s.shape, s.dtype) for s in shapes] + [dma((places,)), dma((places,))],
            compiler_params=pltpu.CompilerParams(vmem_limit_bytes=most),
            name="results",
        )(*new)

    tokens, whole = P(("rep", "dp"), None, None), P(None, None, None)
    shares = [P(None, "dp", None)] * 6
    return jax.shard_map(
        step,
        mesh=mesh,
        in_specs=(tokens, tokens, whole, whole, whole, *shares),
        out_specs=tuple([P("rep", None, None)] * 3 + [P("rep", "dp", None)] * 6),
        check_vma=False,
    )
```

time: 405 us -> 360 us (0.89)
  local copies, waits for them, and re-layouts: 27.1 us -> 0 us
  Pallas kernels: 377 us -> 359 us
    unnamed x27 -> x0, local copies, waits for them, and re-layouts: 27.1 us -> none
    pallas_call x1 -> x2, Pallas kernels: 377 us -> 359 us  [the longest x1 338 us: step(): pl.pallas_call(functools.partial(kernel, n), out_shape=shapes, in_specs=[...]
where the time goes in v2:
time: 360 us
  Pallas kernels  359 us (100%)
    pallas_call x1, Pallas kernels, step(): pl.pallas_call(functools.partial(kernel, n), out_shape=shapes, in_specs=[...  338 us
    pallas_call x1, Pallas kernels, step(): pl.pallas_call(copies, out_shape=shapes, in_specs=[anywhere] * 9, out_spe...  21.4 us

profile of v2, /device:TPU:112, one launch (start us, length us, event | category | flops | bytes accessed | tf_op | source)
XLA Modules:
  0.0 360.0 jit_solution(8249157753728765055)
XLA Ops:
  0.6 337.8 %train_step.1 = (bf16[2,640,2048]{2,1,0:T(8,128)(2,1)}, bf16[2,640,2048]{2,1,0:T(8,128)(2,1)}, bf16[2,2048,640]{2,1,0:T(8,128)(2,1)}, f32[2,160,2048]{2,1,0:T(8,...) custom-call(bf16[1,4096,640]{2,1,0:T(8,128)(2,1)} %x_in.1, ...), custom_call_target="tpu_custom_call" | custom-call | tf_op jit(solution)/shard_map/train_step/pallas_call | solution.py:424
  338.5 21.4 %results.1 = (bf16[2,640,2048]{2,1,0:T(8,128)(2,1)}, bf16[2,640,2048]{2,1,0:T(8,128)(2,1)}, bf16[2,2048,640]{2,1,0:T(8,128)(2,1)}, f32[2,160,2048]{2,1,0:T(8,128...) custom-call(bf16[2,640,2048]{2,1,0:T(8,128)(2,1)} %get-tuple-element, ...), custom_call_target="tpu_custom_call" | custom-call | tf_op jit(solution)/shard_map/results/pallas_call | solution.py:469
